TPU v7x, 32 devices: a whole 2x2x4 slice. The times are simulated.
32 devices in a mesh: row: 4 (over y, x), col: 8 (over z, core).
Axes of the slice: x: 2, y: 2, z: 4, core: 2. Of those that a mesh axis runs over, the one named last changes fastest.
Arguments:
- depth: float32 [256, 4096], P('row', 'col'), may hold values from 0 to 1
- rainfall: float32 [256, 4096], P('row', 'col'), may hold values from 0.05 to 0.5
- conveyance: float32 [256, 4096], P('row', 'col'), may hold values from 0.2 to 5
- flow_dir: int32 [256, 4096], P('row', 'col'), may hold values from 0 to 7, as said below
- outlet: int32 [256, 4096], P('row', 'col'), may hold values 0 or 1
Outputs:
- new_depth: float32 [256, 4096], P('row', 'col')
- discharge: float32 [256, 4096], P('row', 'col')
Inputs may be any that keep to these rules, and one draw needn't show every extreme that they name: `flow_dir`: each cell's code is 0 to 7.
All inputs are finite; a program needn't handle non-finite values. No bound on the sum of `outlet` on one device may be relied on, other than what follows from the above.
Results may differ from a plain program's by a relative error of at most 0.00002.
Values sent between devices are 32-bit elements; how exact they have to be, the bound alone decides.
No kernel may reach another device: no remote copies, remote signals or barrier semaphores. Data moves between devices by JAX's collectives and lax.ppermute only.
A program may use at most 64 MiB of HBM per device.

v0:
```python
import jax
import jax.numpy as jnp
from jax import lax
from jax.sharding import PartitionSpec as P

SUBSTEPS = 3
PASSES = 64


OFFSETS = ((0, 1), (1, 1), (1, 0), (1, -1), (0, -1), (-1, -1), (-1, 0), (-1, 1))


def extended(array, sides, width):
    for axis, dim in sides:
        peers, length = (lax.axis_size(axis), array.shape[dim])
        up = [(i, (i + 1) % peers) for i in range(peers - 1)]
        down = [(j, i) for i, j in up]
        last = lax.slice_in_dim(array, length - width, length, axis=dim)
        initial = lax.slice_in_dim(array, 0, width, axis=dim)
        before = lax.ppermute(last, axis, up)
        after = lax.ppermute(initial, axis, down)
        array = jnp.concatenate([before, array, after], axis=dim)
    return array


def padded_inflow(sent_pad, route_pad):
    rows = sent_pad.shape[0] - 2
    cols = sent_pad.shape[1] - 2
    total = jnp.zeros((rows, cols), jnp.float32)
    for k, (di, dj) in enumerate(OFFSETS):
        source = sent_pad[1 - di : 1 - di + rows, 1 - dj : 1 - dj + cols]
        target = route_pad[1 - di : 1 - di + rows, 1 - dj : 1 - dj + cols]
        total = total + jnp.where(target == k + 1, source, jnp.float32(0.0))
    return total


def on_device(depth, rainfall, conveyance, flow_dir, outlet):
    route = jnp.where(outlet == 1, 0, flow_dir + 1)
    length = jnp.where(flow_dir % 2 == 1, jnp.float32(0.70710678), jnp.float32(1.0))
    route_pad = extended(route, (("row", 0), ("col", 1)), 1)
    level = depth
    for step in range(SUBSTEPS):
        factor = conveyance * length * jnp.power(level, jnp.float32(2.0 / 3.0))
        share = factor / (1.0 + factor)
        out = level * share
        sent = jnp.where(route > 0, out, jnp.float32(0.0))
        sent_pad = extended(sent, (("row", 0), ("col", 1)), 1)
        level = level + rainfall - out + padded_inflow(sent_pad, route_pad)
    margin = 8
    route_wide = extended(route, (("row", 0), ("col", 1)), margin)
    level_wide = extended(level, (("row", 0), ("col", 1)), margin)
    rows, cols = level.shape

    def group_pass(index, acc):
        current = extended(acc, (("row", 0), ("col", 1)), margin)
        for inner in range(margin):
            edge = margin - inner
            route_here = route_wide[
                margin - edge : margin + rows + edge, margin - edge : margin + cols + edge
            ]
            level_here = level_wide[
                margin - edge + 1 : margin + rows + edge - 1,
                margin - edge + 1 : margin + cols + edge - 1,
            ]
            sent = jnp.where(route_here > 0, current, jnp.float32(0.0))
            current = level_here + padded_inflow(sent, route_here)
        return current

    acc = lax.fori_loop(0, PASSES // margin, group_pass, level)
    return (level, jnp.log(1.0 + acc))


def solution(mesh):
    placed = (P("row", "col"), P("row", "col"), P("row", "col"), P("row", "col"), P("row", "col"))
    return jax.shard_map(
        on_device,
        mesh=mesh,
        in_specs=placed,
        out_specs=(P("row", "col"), P("row", "col")),
        check_vma=False,
    )
```

profile of v0, /device:TPU:0, one launch (start us, length us, event | category | flops | bytes accessed | tf_op | source)
XLA Modules:
  0.0 261.8 jit_solution(14108373499394665814)
XLA Ops:
  2.0 4.9 %collective-permute-start.4 = (s32[1,512]{1,0:T(1,128)S(1)}, s32[1,512]{1,0:T(1,128)S(1)}, u32[]{:S(2)}, u32[]{:S(2)}) collective-permute-start(s32[1,512]{1,0:T(1,128)S(1)} %get-tuple-element.88), channel_id=1, source_target_pairs={{0,8},{8,16},{16,24},{1,9},{9,17},{17,25},{2,10},{10,18},{18,26},{... | collective-permute-start | bytes 6152 | tf_op jit(solution)/shard_map/ppermute | solution.py:20
  8.2 4.5 %collective-permute-start.7 = (f32[1,512]{1,0:T(1,128)S(1)}, f32[1,512]{1,0:T(1,128)S(1)}, u32[]{:S(2)}, u32[]{:S(2)}) collective-permute-start(f32[1,512]{1,0:T(1,128)S(1)} %get-tuple-element.90), channel_id=1, source_target_pairs={{0,8},{8,16},{16,24},{1,9},{9,17},{17,25},{2,10},{10,18},{18,26},{... | collective-permute-start | bytes 6152 | tf_op jit(solution)/shard_map/ppermute | solution.py:20
  20.0 3.6 %collective-permute-start.9 = (f32[66,1]{1,0:T(8,128)S(1)}, f32[66,1]{1,0:T(8,128)S(1)}, u32[]{:S(2)}, u32[]{:S(2)}) collective-permute-start(f32[66,1]{1,0:T(8,128)S(1)} %get-tuple-element.79), channel_id=1, source_target_pairs={{0,1},{1,2},{2,3},{3,4},{4,5},{5,6},{6,7},{8,9},{9,10},{10,11},{11... | collective-permute-start | bytes 800 | tf_op jit(solution)/shard_map/ppermute | solution.py:20
  25.5 4.9 %collective-permute-start.12 = (f32[1,512]{1,0:T(1,128)S(1)}, f32[1,512]{1,0:T(1,128)S(1)}, u32[]{:S(2)}, u32[]{:S(2)}) collective-permute-start(f32[1,512]{1,0:T(1,128)S(1)} %get-tuple-element.86), channel_id=1, source_target_pairs={{0,8},{8,16},{16,24},{1,9},{9,17},{17,25},{2,10},{10,18},{18,26},{... | collective-permute-start | bytes 6152 | tf_op jit(solution)/shard_map/ppermute | solution.py:20
  31.7 5.1 %collective-permute-done.13 = f32[1,512]{1,0:T(1,128)S(1)} collective-permute-done((f32[1,512]{1,0:T(1,128)S(1)}, f32[1,512]{1,0:T(1,128)S(1)}, u32[]{:S(2)}, u32[]{:S(2)}) %collective-permute-start.13) | collective-permute-done | bytes 2080 | tf_op jit(solution)/shard_map/ppermute | solution.py:21
  40.8 4.8 %collective-permute-done.15 = f32[66,1]{1,0:T(8,128)S(1)} collective-permute-done((f32[66,1]{1,0:T(8,128)S(1)}, f32[66,1]{1,0:T(8,128)S(1)}, u32[]{:S(2)}, u32[]{:S(2)}) %collective-permute-start.15) | collective-permute-done | bytes 296 | tf_op jit(solution)/shard_map/ppermute | solution.py:21
  46.3 4.8 %collective-permute-start.16 = (f32[1,512]{1,0:T(1,128)S(1)}, f32[1,512]{1,0:T(1,128)S(1)}, u32[]{:S(2)}, u32[]{:S(2)}) collective-permute-start(f32[1,512]{1,0:T(1,128)S(1)} %get-tuple-element.84), channel_id=1, source_target_pairs={{0,8},{8,16},{16,24},{1,9},{9,17},{17,25},{2,10},{10,18},{18,26},{... | collective-permute-start | bytes 6152 | tf_op jit(solution)/shard_map/ppermute | solution.py:20
  52.4 4.5 %collective-permute-start.20 = (s32[8,512]{1,0:T(8,128)S(1)}, s32[8,512]{1,0:T(8,128)S(1)}, u32[]{:S(2)}, u32[]{:S(2)}) collective-permute-start(s32[8,512]{1,0:T(8,128)S(1)} %get-tuple-element.82), channel_id=1, source_target_pairs={{0,8},{8,16},{16,24},{1,9},{9,17},{17,25},{2,10},{10,18},{18,26},{... | collective-permute-start | bytes 49160 | tf_op jit(solution)/shard_map/ppermute | solution.py:20
  57.1 3.7 %collective-permute-start.18 = (f32[66,1]{1,0:T(8,128)S(1)}, f32[66,1]{1,0:T(8,128)S(1)}, u32[]{:S(2)}, u32[]{:S(2)}) collective-permute-start(f32[66,1]{1,0:T(8,128)S(1)} %get-tuple-element.67), channel_id=1, source_target_pairs={{0,1},{1,2},{2,3},{3,4},{4,5},{5,6},{6,7},{8,9},{9,10},{10,11},{11... | collective-permute-start | bytes 800 | tf_op jit(solution)/shard_map/ppermute | solution.py:20
  64.8 3.7 %collective-permute-start.24 = (f32[8,512]{1,0:T(8,128)S(1)}, f32[8,512]{1,0:T(8,128)S(1)}, u32[]{:S(2)}, u32[]{:S(2)}) collective-permute-start(f32[8,512]{1,0:T(8,128)S(1)} %get-tuple-element.80), channel_id=1, source_target_pairs={{0,8},{8,16},{16,24},{1,9},{9,17},{17,25},{2,10},{10,18},{18,26},{... | collective-permute-start | bytes 49160 | tf_op jit(solution)/shard_map/ppermute | solution.py:20
  69.9 3.4 %collective-permute-start.22 = (s32[80,8]{1,0:T(8,128)S(1)}, s32[80,8]{1,0:T(8,128)S(1)}, u32[]{:S(2)}, u32[]{:S(2)}) collective-permute-start(s32[80,8]{1,0:T(8,128)S(1)} %get-tuple-element.62), channel_id=1, source_target_pairs={{0,1},{1,2},{2,3},{3,4},{4,5},{5,6},{6,7},{8,9},{9,10},{10,11},{11... | collective-permute-start | bytes 7688 | tf_op jit(solution)/shard_map/ppermute | solution.py:20
  74.7 4.2 %collective-permute-start.26 = (f32[80,8]{1,0:T(8,128)S(1)}, f32[80,8]{1,0:T(8,128)S(1)}, u32[]{:S(2)}, u32[]{:S(2)}) collective-permute-start(f32[80,8]{1,0:T(8,128)S(1)} %get-tuple-element.60), channel_id=1, source_target_pairs={{0,1},{1,2},{2,3},{3,4},{4,5},{5,6},{6,7},{8,9},{9,10},{10,11},{11... | collective-permute-start | bytes 7688 | tf_op jit(solution)/shard_map/ppermute | solution.py:20
  83.5 177.6 %while.10 = (s32[]{:T(128)}, f32[64,512]{1,0:T(8,128)S(1)}, s32[80,528]{1,0:T(8,128)S(1)}, f32[80,528]{1,0:T(8,128)S(1)}, f32[64,512]{1,0:T(8,128)S(1)}, /*index=5*/s32[]{:T(128)}) while((s32[]{:T(128)}, f32[64,512]{1,0:T(8,128)S(1)}, s32[80,528]{1,0:T(8,128)S(1)}, f32[80,528]{1,0:T(8,128)S(1)}, f32[64,512]{1,0:T(8,128)S(1)}, ...), condition=%wide.region_1.2_spmd, body=%wide.region_0.1_spmd.sunk | while | flops 7772386 | bytes 23348004 | solution.py:69
  83.5 4.5 %collective-permute-start = (f32[8,512]{1,0:T(8,128)S(1)}, f32[8,512]{1,0:T(8,128)S(1)}, u32[]{:S(2)}, u32[]{:S(2)}) collective-permute-start(f32[8,512]{1,0:T(8,128)S(1)} %get-tuple-element.127), channel_id=1, source_target_pairs={{0,8},{8,16},{16,24},{1,9},{9,17},{17,25},{2,10},{10,18},{18,26},{... | collective-permute-start | bytes 49160 | tf_op jit(solution)/shard_map/while/body/eval_jaxpr/ppermute | solution.py:20
  89.5 4.9 %collective-permute-done.1 = f32[8,512]{1,0:T(8,128)S(1)} collective-permute-done((f32[8,512]{1,0:T(8,128)S(1)}, f32[8,512]{1,0:T(8,128)S(1)}, u32[]{:S(2)}, u32[]{:S(2)}) %collective-permute-start.1) | collective-permute-done | bytes 16416 | tf_op jit(solution)/shard_map/while/body/eval_jaxpr/ppermute | solution.py:21
  95.8 4.1 %collective-permute-start.3 = (f32[80,8]{1,0:T(8,128)S(1)}, f32[80,8]{1,0:T(8,128)S(1)}, u32[]{:S(2)}, u32[]{:S(2)}) collective-permute-start(f32[80,8]{1,0:T(8,128)S(1)} %get-tuple-element.130), channel_id=1, source_target_pairs={{0,1},{1,2},{2,3},{3,4},{4,5},{5,6},{6,7},{8,9},{9,10},{10,11},{11... | collective-permute-start | bytes 7688 | tf_op jit(solution)/shard_map/while/body/eval_jaxpr/ppermute | solution.py:20
  107.0 4.5 %collective-permute-start = (f32[8,512]{1,0:T(8,128)S(1)}, f32[8,512]{1,0:T(8,128)S(1)}, u32[]{:S(2)}, u32[]{:S(2)}) collective-permute-start(f32[8,512]{1,0:T(8,128)S(1)} %get-tuple-element.127), channel_id=1, source_target_pairs={{0,8},{8,16},{16,24},{1,9},{9,17},{17,25},{2,10},{10,18},{18,26},{... | collective-permute-start | bytes 49160 | tf_op jit(solution)/shard_map/while/body/eval_jaxpr/ppermute | solution.py:20
  113.0 4.2 %collective-permute-done.1 = f32[8,512]{1,0:T(8,128)S(1)} collective-permute-done((f32[8,512]{1,0:T(8,128)S(1)}, f32[8,512]{1,0:T(8,128)S(1)}, u32[]{:S(2)}, u32[]{:S(2)}) %collective-permute-start.1) | collective-permute-done | bytes 16416 | tf_op jit(solution)/shard_map/while/body/eval_jaxpr/ppermute | solution.py:21
  128.7 3.1 %collective-permute-start = (f32[8,512]{1,0:T(8,128)S(1)}, f32[8,512]{1,0:T(8,128)S(1)}, u32[]{:S(2)}, u32[]{:S(2)}) collective-permute-start(f32[8,512]{1,0:T(8,128)S(1)} %get-tuple-element.127), channel_id=1, source_target_pairs={{0,8},{8,16},{16,24},{1,9},{9,17},{17,25},{2,10},{10,18},{18,26},{... | collective-permute-start | bytes 49160 | tf_op jit(solution)/shard_map/while/body/eval_jaxpr/ppermute | solution.py:20
  133.3 4.2 %collective-permute-done.1 = f32[8,512]{1,0:T(8,128)S(1)} collective-permute-done((f32[8,512]{1,0:T(8,128)S(1)}, f32[8,512]{1,0:T(8,128)S(1)}, u32[]{:S(2)}, u32[]{:S(2)}) %collective-permute-start.1) | collective-permute-done | bytes 16416 | tf_op jit(solution)/shard_map/while/body/eval_jaxpr/ppermute | solution.py:21
  138.9 4.8 %collective-permute-start.3 = (f32[80,8]{1,0:T(8,128)S(1)}, f32[80,8]{1,0:T(8,128)S(1)}, u32[]{:S(2)}, u32[]{:S(2)}) collective-permute-start(f32[80,8]{1,0:T(8,128)S(1)} %get-tuple-element.130), channel_id=1, source_target_pairs={{0,1},{1,2},{2,3},{3,4},{4,5},{5,6},{6,7},{8,9},{9,10},{10,11},{11... | collective-permute-start | bytes 7688 | tf_op jit(solution)/shard_map/while/body/eval_jaxpr/ppermute | solution.py:20
  150.8 3.1 %collective-permute-start = (f32[8,512]{1,0:T(8,128)S(1)}, f32[8,512]{1,0:T(8,128)S(1)}, u32[]{:S(2)}, u32[]{:S(2)}) collective-permute-start(f32[8,512]{1,0:T(8,128)S(1)} %get-tuple-element.127), channel_id=1, source_target_pairs={{0,8},{8,16},{16,24},{1,9},{9,17},{17,25},{2,10},{10,18},{18,26},{... | collective-permute-start | bytes 49160 | tf_op jit(solution)/shard_map/while/body/eval_jaxpr/ppermute | solution.py:20
  155.4 4.2 %collective-permute-done.1 = f32[8,512]{1,0:T(8,128)S(1)} collective-permute-done((f32[8,512]{1,0:T(8,128)S(1)}, f32[8,512]{1,0:T(8,128)S(1)}, u32[]{:S(2)}, u32[]{:S(2)}) %collective-permute-start.1) | collective-permute-done | bytes 16416 | tf_op jit(solution)/shard_map/while/body/eval_jaxpr/ppermute | solution.py:21
  160.9 4.8 %collective-permute-start.3 = (f32[80,8]{1,0:T(8,128)S(1)}, f32[80,8]{1,0:T(8,128)S(1)}, u32[]{:S(2)}, u32[]{:S(2)}) collective-permute-start(f32[80,8]{1,0:T(8,128)S(1)} %get-tuple-element.130), channel_id=1, source_target_pairs={{0,1},{1,2},{2,3},{3,4},{4,5},{5,6},{6,7},{8,9},{9,10},{10,11},{11... | collective-permute-start | bytes 7688 | tf_op jit(solution)/shard_map/while/body/eval_jaxpr/ppermute | solution.py:20
  177.4 4.2 %collective-permute-done.1 = f32[8,512]{1,0:T(8,128)S(1)} collective-permute-done((f32[8,512]{1,0:T(8,128)S(1)}, f32[8,512]{1,0:T(8,128)S(1)}, u32[]{:S(2)}, u32[]{:S(2)}) %collective-permute-start.1) | collective-permute-done | bytes 16416 | tf_op jit(solution)/shard_map/while/body/eval_jaxpr/ppermute | solution.py:21
  183.0 4.8 %collective-permute-start.3 = (f32[80,8]{1,0:T(8,128)S(1)}, f32[80,8]{1,0:T(8,128)S(1)}, u32[]{:S(2)}, u32[]{:S(2)}) collective-permute-start(f32[80,8]{1,0:T(8,128)S(1)} %get-tuple-element.130), channel_id=1, source_target_pairs={{0,1},{1,2},{2,3},{3,4},{4,5},{5,6},{6,7},{8,9},{9,10},{10,11},{11... | collective-permute-start | bytes 7688 | tf_op jit(solution)/shard_map/while/body/eval_jaxpr/ppermute | solution.py:20
  199.5 4.2 %collective-permute-done.1 = f32[8,512]{1,0:T(8,128)S(1)} collective-permute-done((f32[8,512]{1,0:T(8,128)S(1)}, f32[8,512]{1,0:T(8,128)S(1)}, u32[]{:S(2)}, u32[]{:S(2)}) %collective-permute-start.1) | collective-permute-done | bytes 16416 | tf_op jit(solution)/shard_map/while/body/eval_jaxpr/ppermute | solution.py:21
  205.0 4.8 %collective-permute-start.3 = (f32[80,8]{1,0:T(8,128)S(1)}, f32[80,8]{1,0:T(8,128)S(1)}, u32[]{:S(2)}, u32[]{:S(2)}) collective-permute-start(f32[80,8]{1,0:T(8,128)S(1)} %get-tuple-element.130), channel_id=1, source_target_pairs={{0,1},{1,2},{2,3},{3,4},{4,5},{5,6},{6,7},{8,9},{9,10},{10,11},{11... | collective-permute-start | bytes 7688 | tf_op jit(solution)/shard_map/while/body/eval_jaxpr/ppermute | solution.py:20
  221.5 4.2 %collective-permute-done.1 = f32[8,512]{1,0:T(8,128)S(1)} collective-permute-done((f32[8,512]{1,0:T(8,128)S(1)}, f32[8,512]{1,0:T(8,128)S(1)}, u32[]{:S(2)}, u32[]{:S(2)}) %collective-permute-start.1) | collective-permute-done | bytes 16416 | tf_op jit(solution)/shard_map/while/body/eval_jaxpr/ppermute | solution.py:21
  227.1 4.8 %collective-permute-start.3 = (f32[80,8]{1,0:T(8,128)S(1)}, f32[80,8]{1,0:T(8,128)S(1)}, u32[]{:S(2)}, u32[]{:S(2)}) collective-permute-start(f32[80,8]{1,0:T(8,128)S(1)} %get-tuple-element.130), channel_id=1, source_target_pairs={{0,1},{1,2},{2,3},{3,4},{4,5},{5,6},{6,7},{8,9},{9,10},{10,11},{11... | collective-permute-start | bytes 7688 | tf_op jit(solution)/shard_map/while/body/eval_jaxpr/ppermute | solution.py:20
  243.6 4.2 %collective-permute-done.1 = f32[8,512]{1,0:T(8,128)S(1)} collective-permute-done((f32[8,512]{1,0:T(8,128)S(1)}, f32[8,512]{1,0:T(8,128)S(1)}, u32[]{:S(2)}, u32[]{:S(2)}) %collective-permute-start.1) | collective-permute-done | bytes 16416 | tf_op jit(solution)/shard_map/while/body/eval_jaxpr/ppermute | solution.py:21
  249.2 4.8 %collective-permute-start.3 = (f32[80,8]{1,0:T(8,128)S(1)}, f32[80,8]{1,0:T(8,128)S(1)}, u32[]{:S(2)}, u32[]{:S(2)}) collective-permute-start(f32[80,8]{1,0:T(8,128)S(1)} %get-tuple-element.130), channel_id=1, source_target_pairs={{0,1},{1,2},{2,3},{3,4},{4,5},{5,6},{6,7},{8,9},{9,10},{10,11},{11... | collective-permute-start | bytes 7688 | tf_op jit(solution)/shard_map/while/body/eval_jaxpr/ppermute | solution.py:20
  (223 shorter events, 124.9 us)
Async XLA Ops:
  2.0 12.0 %collective-permute-start.4 = (s32[1,512]{1,0:T(1,128)S(1)}, s32[1,512]{1,0:T(1,128)S(1)}, u32[]{:S(2)}, u32[]{:S(2)}) collective-permute-start(s32[1,512]{1,0:T(1,128)S(1)} %get-tuple-element.88), channel_id=1, source_target_pairs={{0,8},{8,16},{16,24},{1,9},{9,17},{17,25},{2,10},{10,18},{18,26},{... | collective-permute-start | bytes 6152 | tf_op jit(solution)/shard_map/ppermute | solution.py:20
  6.9 7.2 %collective-permute-start.5 = (s32[1,512]{1,0:T(1,128)S(1)}, s32[1,512]{1,0:T(1,128)S(1)}, u32[]{:S(2)}, u32[]{:S(2)}) collective-permute-start(s32[1,512]{1,0:T(1,128)S(1)} %get-tuple-element.89), channel_id=1, source_target_pairs={{8,0},{16,8},{24,16},{9,1},{17,9},{25,17},{10,2},{18,10},{26,18},{... | collective-permute-start | bytes 6152 | tf_op jit(solution)/shard_map/ppermute | solution.py:21
  8.2 10.3 %collective-permute-start.7 = (f32[1,512]{1,0:T(1,128)S(1)}, f32[1,512]{1,0:T(1,128)S(1)}, u32[]{:S(2)}, u32[]{:S(2)}) collective-permute-start(f32[1,512]{1,0:T(1,128)S(1)} %get-tuple-element.90), channel_id=1, source_target_pairs={{0,8},{8,16},{16,24},{1,9},{9,17},{17,25},{2,10},{10,18},{18,26},{... | collective-permute-start | bytes 6152 | tf_op jit(solution)/shard_map/ppermute | solution.py:20
  12.7 5.9 %collective-permute-start.8 = (f32[1,512]{1,0:T(1,128)S(1)}, f32[1,512]{1,0:T(1,128)S(1)}, u32[]{:S(2)}, u32[]{:S(2)}) collective-permute-start(f32[1,512]{1,0:T(1,128)S(1)} %get-tuple-element.91), channel_id=1, source_target_pairs={{8,0},{16,8},{24,16},{9,1},{17,9},{25,17},{10,2},{18,10},{26,18},{... | collective-permute-start | bytes 6152 | tf_op jit(solution)/shard_map/ppermute | solution.py:21
  14.2 9.5 %collective-permute-start.10 = (s32[66,1]{1,0:T(8,128)S(1)}, s32[66,1]{1,0:T(8,128)S(1)}, u32[]{:S(2)}, u32[]{:S(2)}) collective-permute-start(s32[66,1]{1,0:T(8,128)S(1)} %get-tuple-element.74), channel_id=1, source_target_pairs={{1,0},{2,1},{3,2},{4,3},{5,4},{6,5},{7,6},{9,8},{10,9},{11,10},{12... | collective-permute-start | bytes 800 | tf_op jit(solution)/shard_map/ppermute | solution.py:21
  15.4 8.2 %collective-permute-start.6 = (s32[66,1]{1,0:T(8,128)S(1)}, s32[66,1]{1,0:T(8,128)S(1)}, u32[]{:S(2)}, u32[]{:S(2)}) collective-permute-start(s32[66,1]{1,0:T(8,128)S(1)} %get-tuple-element.75), channel_id=1, source_target_pairs={{0,1},{1,2},{2,3},{3,4},{4,5},{5,6},{6,7},{8,9},{9,10},{10,11},{11... | collective-permute-start | bytes 800 | tf_op jit(solution)/shard_map/ppermute | solution.py:20
  25.5 6.2 %collective-permute-start.12 = (f32[1,512]{1,0:T(1,128)S(1)}, f32[1,512]{1,0:T(1,128)S(1)}, u32[]{:S(2)}, u32[]{:S(2)}) collective-permute-start(f32[1,512]{1,0:T(1,128)S(1)} %get-tuple-element.86), channel_id=1, source_target_pairs={{0,8},{8,16},{16,24},{1,9},{9,17},{17,25},{2,10},{10,18},{18,26},{... | collective-permute-start | bytes 6152 | tf_op jit(solution)/shard_map/ppermute | solution.py:20
  30.4 6.4 %collective-permute-start.13 = (f32[1,512]{1,0:T(1,128)S(1)}, f32[1,512]{1,0:T(1,128)S(1)}, u32[]{:S(2)}, u32[]{:S(2)}) collective-permute-start(f32[1,512]{1,0:T(1,128)S(1)} %get-tuple-element.87), channel_id=1, source_target_pairs={{8,0},{16,8},{24,16},{9,1},{17,9},{25,17},{10,2},{18,10},{26,18},{... | collective-permute-start | bytes 6152 | tf_op jit(solution)/shard_map/ppermute | solution.py:21
  39.5 6.1 %collective-permute-start.15 = (f32[66,1]{1,0:T(8,128)S(1)}, f32[66,1]{1,0:T(8,128)S(1)}, u32[]{:S(2)}, u32[]{:S(2)}) collective-permute-start(f32[66,1]{1,0:T(8,128)S(1)} %get-tuple-element.70), channel_id=1, source_target_pairs={{1,0},{2,1},{3,2},{4,3},{5,4},{6,5},{7,6},{9,8},{10,9},{11,10},{12... | collective-permute-start | bytes 800 | tf_op jit(solution)/shard_map/ppermute | solution.py:21
  46.3 10.7 %collective-permute-start.16 = (f32[1,512]{1,0:T(1,128)S(1)}, f32[1,512]{1,0:T(1,128)S(1)}, u32[]{:S(2)}, u32[]{:S(2)}) collective-permute-start(f32[1,512]{1,0:T(1,128)S(1)} %get-tuple-element.84), channel_id=1, source_target_pairs={{0,8},{8,16},{16,24},{1,9},{9,17},{17,25},{2,10},{10,18},{18,26},{... | collective-permute-start | bytes 6152 | tf_op jit(solution)/shard_map/ppermute | solution.py:20
  51.1 5.9 %collective-permute-start.17 = (f32[1,512]{1,0:T(1,128)S(1)}, f32[1,512]{1,0:T(1,128)S(1)}, u32[]{:S(2)}, u32[]{:S(2)}) collective-permute-start(f32[1,512]{1,0:T(1,128)S(1)} %get-tuple-element.85), channel_id=1, source_target_pairs={{8,0},{16,8},{24,16},{9,1},{17,9},{25,17},{10,2},{18,10},{26,18},{... | collective-permute-start | bytes 6152 | tf_op jit(solution)/shard_map/ppermute | solution.py:21
  52.4 17.4 %collective-permute-start.20 = (s32[8,512]{1,0:T(8,128)S(1)}, s32[8,512]{1,0:T(8,128)S(1)}, u32[]{:S(2)}, u32[]{:S(2)}) collective-permute-start(s32[8,512]{1,0:T(8,128)S(1)} %get-tuple-element.82), channel_id=1, source_target_pairs={{0,8},{8,16},{16,24},{1,9},{9,17},{17,25},{2,10},{10,18},{18,26},{... | collective-permute-start | bytes 49160 | tf_op jit(solution)/shard_map/ppermute | solution.py:20
  57.1 6.3 %collective-permute-start.18 = (f32[66,1]{1,0:T(8,128)S(1)}, f32[66,1]{1,0:T(8,128)S(1)}, u32[]{:S(2)}, u32[]{:S(2)}) collective-permute-start(f32[66,1]{1,0:T(8,128)S(1)} %get-tuple-element.67), channel_id=1, source_target_pairs={{0,1},{1,2},{2,3},{3,4},{4,5},{5,6},{6,7},{8,9},{9,10},{10,11},{11... | collective-permute-start | bytes 800 | tf_op jit(solution)/shard_map/ppermute | solution.py:20
  62.1 7.8 %collective-permute-start.21 = (s32[8,512]{1,0:T(8,128)S(1)}, s32[8,512]{1,0:T(8,128)S(1)}, u32[]{:S(2)}, u32[]{:S(2)}) collective-permute-start(s32[8,512]{1,0:T(8,128)S(1)} %get-tuple-element.83), channel_id=1, source_target_pairs={{8,0},{16,8},{24,16},{9,1},{17,9},{25,17},{10,2},{18,10},{26,18},{... | collective-permute-start | bytes 49160 | tf_op jit(solution)/shard_map/ppermute | solution.py:21
  64.8 9.8 %collective-permute-start.24 = (f32[8,512]{1,0:T(8,128)S(1)}, f32[8,512]{1,0:T(8,128)S(1)}, u32[]{:S(2)}, u32[]{:S(2)}) collective-permute-start(f32[8,512]{1,0:T(8,128)S(1)} %get-tuple-element.80), channel_id=1, source_target_pairs={{0,8},{8,16},{16,24},{1,9},{9,17},{17,25},{2,10},{10,18},{18,26},{... | collective-permute-start | bytes 49160 | tf_op jit(solution)/shard_map/ppermute | solution.py:20
  68.5 6.1 %collective-permute-start.25 = (f32[8,512]{1,0:T(8,128)S(1)}, f32[8,512]{1,0:T(8,128)S(1)}, u32[]{:S(2)}, u32[]{:S(2)}) collective-permute-start(f32[8,512]{1,0:T(8,128)S(1)} %get-tuple-element.81), channel_id=1, source_target_pairs={{8,0},{16,8},{24,16},{9,1},{17,9},{25,17},{10,2},{18,10},{26,18},{... | collective-permute-start | bytes 49160 | tf_op jit(solution)/shard_map/ppermute | solution.py:21
  69.9 10.3 %collective-permute-start.22 = (s32[80,8]{1,0:T(8,128)S(1)}, s32[80,8]{1,0:T(8,128)S(1)}, u32[]{:S(2)}, u32[]{:S(2)}) collective-permute-start(s32[80,8]{1,0:T(8,128)S(1)} %get-tuple-element.62), channel_id=1, source_target_pairs={{0,1},{1,2},{2,3},{3,4},{4,5},{5,6},{6,7},{8,9},{9,10},{10,11},{11... | collective-permute-start | bytes 7688 | tf_op jit(solution)/shard_map/ppermute | solution.py:20
  73.3 7.0 %collective-permute-start.23 = (s32[80,8]{1,0:T(8,128)S(1)}, s32[80,8]{1,0:T(8,128)S(1)}, u32[]{:S(2)}, u32[]{:S(2)}) collective-permute-start(s32[80,8]{1,0:T(8,128)S(1)} %get-tuple-element.63), channel_id=1, source_target_pairs={{1,0},{2,1},{3,2},{4,3},{5,4},{6,5},{7,6},{9,8},{10,9},{11,10},{12... | collective-permute-start | bytes 7688 | tf_op jit(solution)/shard_map/ppermute | solution.py:21
  74.7 5.7 %collective-permute-start.26 = (f32[80,8]{1,0:T(8,128)S(1)}, f32[80,8]{1,0:T(8,128)S(1)}, u32[]{:S(2)}, u32[]{:S(2)}) collective-permute-start(f32[80,8]{1,0:T(8,128)S(1)} %get-tuple-element.60), channel_id=1, source_target_pairs={{0,1},{1,2},{2,3},{3,4},{4,5},{5,6},{6,7},{8,9},{9,10},{10,11},{11... | collective-permute-start | bytes 7688 | tf_op jit(solution)/shard_map/ppermute | solution.py:20
  83.5 6.0 %collective-permute-start = (f32[8,512]{1,0:T(8,128)S(1)}, f32[8,512]{1,0:T(8,128)S(1)}, u32[]{:S(2)}, u32[]{:S(2)}) collective-permute-start(f32[8,512]{1,0:T(8,128)S(1)} %get-tuple-element.127), channel_id=1, source_target_pairs={{0,8},{8,16},{16,24},{1,9},{9,17},{17,25},{2,10},{10,18},{18,26},{... | collective-permute-start | bytes 49160 | tf_op jit(solution)/shard_map/while/body/eval_jaxpr/ppermute | solution.py:20
  88.1 6.3 %collective-permute-start.1 = (f32[8,512]{1,0:T(8,128)S(1)}, f32[8,512]{1,0:T(8,128)S(1)}, u32[]{:S(2)}, u32[]{:S(2)}) collective-permute-start(f32[8,512]{1,0:T(8,128)S(1)} %get-tuple-element.128), channel_id=1, source_target_pairs={{8,0},{16,8},{24,16},{9,1},{17,9},{25,17},{10,2},{18,10},{26,18},{... | collective-permute-start | bytes 49160 | tf_op jit(solution)/shard_map/while/body/eval_jaxpr/ppermute | solution.py:21
  107.0 6.0 %collective-permute-start = (f32[8,512]{1,0:T(8,128)S(1)}, f32[8,512]{1,0:T(8,128)S(1)}, u32[]{:S(2)}, u32[]{:S(2)}) collective-permute-start(f32[8,512]{1,0:T(8,128)S(1)} %get-tuple-element.127), channel_id=1, source_target_pairs={{0,8},{8,16},{16,24},{1,9},{9,17},{17,25},{2,10},{10,18},{18,26},{... | collective-permute-start | bytes 49160 | tf_op jit(solution)/shard_map/while/body/eval_jaxpr/ppermute | solution.py:20
  137.6 6.1 %collective-permute-start.2 = (f32[80,8]{1,0:T(8,128)S(1)}, f32[80,8]{1,0:T(8,128)S(1)}, u32[]{:S(2)}, u32[]{:S(2)}) collective-permute-start(f32[80,8]{1,0:T(8,128)S(1)} %get-tuple-element.129), channel_id=1, source_target_pairs={{1,0},{2,1},{3,2},{4,3},{5,4},{6,5},{7,6},{9,8},{10,9},{11,10},{12... | collective-permute-start | bytes 7688 | tf_op jit(solution)/shard_map/while/body/eval_jaxpr/ppermute | solution.py:21
  138.9 5.7 %collective-permute-start.3 = (f32[80,8]{1,0:T(8,128)S(1)}, f32[80,8]{1,0:T(8,128)S(1)}, u32[]{:S(2)}, u32[]{:S(2)}) collective-permute-start(f32[80,8]{1,0:T(8,128)S(1)} %get-tuple-element.130), channel_id=1, source_target_pairs={{0,1},{1,2},{2,3},{3,4},{4,5},{5,6},{6,7},{8,9},{9,10},{10,11},{11... | collective-permute-start | bytes 7688 | tf_op jit(solution)/shard_map/while/body/eval_jaxpr/ppermute | solution.py:20
  159.6 6.1 %collective-permute-start.2 = (f32[80,8]{1,0:T(8,128)S(1)}, f32[80,8]{1,0:T(8,128)S(1)}, u32[]{:S(2)}, u32[]{:S(2)}) collective-permute-start(f32[80,8]{1,0:T(8,128)S(1)} %get-tuple-element.129), channel_id=1, source_target_pairs={{1,0},{2,1},{3,2},{4,3},{5,4},{6,5},{7,6},{9,8},{10,9},{11,10},{12... | collective-permute-start | bytes 7688 | tf_op jit(solution)/shard_map/while/body/eval_jaxpr/ppermute | solution.py:21
  160.9 5.7 %collective-permute-start.3 = (f32[80,8]{1,0:T(8,128)S(1)}, f32[80,8]{1,0:T(8,128)S(1)}, u32[]{:S(2)}, u32[]{:S(2)}) collective-permute-start(f32[80,8]{1,0:T(8,128)S(1)} %get-tuple-element.130), channel_id=1, source_target_pairs={{0,1},{1,2},{2,3},{3,4},{4,5},{5,6},{6,7},{8,9},{9,10},{10,11},{11... | collective-permute-start | bytes 7688 | tf_op jit(solution)/shard_map/while/body/eval_jaxpr/ppermute | solution.py:20
  181.7 6.1 %collective-permute-start.2 = (f32[80,8]{1,0:T(8,128)S(1)}, f32[80,8]{1,0:T(8,128)S(1)}, u32[]{:S(2)}, u32[]{:S(2)}) collective-permute-start(f32[80,8]{1,0:T(8,128)S(1)} %get-tuple-element.129), channel_id=1, source_target_pairs={{1,0},{2,1},{3,2},{4,3},{5,4},{6,5},{7,6},{9,8},{10,9},{11,10},{12... | collective-permute-start | bytes 7688 | tf_op jit(solution)/shard_map/while/body/eval_jaxpr/ppermute | solution.py:21
  183.0 5.7 %collective-permute-start.3 = (f32[80,8]{1,0:T(8,128)S(1)}, f32[80,8]{1,0:T(8,128)S(1)}, u32[]{:S(2)}, u32[]{:S(2)}) collective-permute-start(f32[80,8]{1,0:T(8,128)S(1)} %get-tuple-element.130), channel_id=1, source_target_pairs={{0,1},{1,2},{2,3},{3,4},{4,5},{5,6},{6,7},{8,9},{9,10},{10,11},{11... | collective-permute-start | bytes 7688 | tf_op jit(solution)/shard_map/while/body/eval_jaxpr/ppermute | solution.py:20
  203.7 6.1 %collective-permute-start.2 = (f32[80,8]{1,0:T(8,128)S(1)}, f32[80,8]{1,0:T(8,128)S(1)}, u32[]{:S(2)}, u32[]{:S(2)}) collective-permute-start(f32[80,8]{1,0:T(8,128)S(1)} %get-tuple-element.129), channel_id=1, source_target_pairs={{1,0},{2,1},{3,2},{4,3},{5,4},{6,5},{7,6},{9,8},{10,9},{11,10},{12... | collective-permute-start | bytes 7688 | tf_op jit(solution)/shard_map/while/body/eval_jaxpr/ppermute | solution.py:21
  205.0 5.7 %collective-permute-start.3 = (f32[80,8]{1,0:T(8,128)S(1)}, f32[80,8]{1,0:T(8,128)S(1)}, u32[]{:S(2)}, u32[]{:S(2)}) collective-permute-start(f32[80,8]{1,0:T(8,128)S(1)} %get-tuple-element.130), channel_id=1, source_target_pairs={{0,1},{1,2},{2,3},{3,4},{4,5},{5,6},{6,7},{8,9},{9,10},{10,11},{11... | collective-permute-start | bytes 7688 | tf_op jit(solution)/shard_map/while/body/eval_jaxpr/ppermute | solution.py:20
  225.8 6.1 %collective-permute-start.2 = (f32[80,8]{1,0:T(8,128)S(1)}, f32[80,8]{1,0:T(8,128)S(1)}, u32[]{:S(2)}, u32[]{:S(2)}) collective-permute-start(f32[80,8]{1,0:T(8,128)S(1)} %get-tuple-element.129), channel_id=1, source_target_pairs={{1,0},{2,1},{3,2},{4,3},{5,4},{6,5},{7,6},{9,8},{10,9},{11,10},{12... | collective-permute-start | bytes 7688 | tf_op jit(solution)/shard_map/while/body/eval_jaxpr/ppermute | solution.py:21
  247.9 6.1 %collective-permute-start.2 = (f32[80,8]{1,0:T(8,128)S(1)}, f32[80,8]{1,0:T(8,128)S(1)}, u32[]{:S(2)}, u32[]{:S(2)}) collective-permute-start(f32[80,8]{1,0:T(8,128)S(1)} %get-tuple-element.129), channel_id=1, source_target_pairs={{1,0},{2,1},{3,2},{4,3},{5,4},{6,5},{7,6},{9,8},{10,9},{11,10},{12... | collective-permute-start | bytes 7688 | tf_op jit(solution)/shard_map/while/body/eval_jaxpr/ppermute | solution.py:21
  (27 other events, 120.4 us)
where the time goes:
time: 267 us; the launch traced here: 262 us
  starting transfers between devices  148 us (55%)
  waiting for transfers between devices  56.4 us (21%)
  other arithmetic  54.4 us (20%)
    ppermute x28, starting transfers between devices, extended(): before = lax.ppermute(last, axis, up)  112 us
    ppermute x28, waiting for transfers between devices, extended(): after = lax.ppermute(initial, axis, down)  48 us
    select_n x64, other arithmetic, group_pass(): sent = jnp.where(route_here > 0, current, jnp.float32(0.0))  45.4 us
    ppermute x28, starting transfers between devices, extended(): after = lax.ppermute(initial, axis, down)  36.1 us
    ppermute x28, waiting for transfers between devices, extended(): before = lax.ppermute(last, axis, up)  8.41 us
  transfers between devices with their start and end apart: 56, of which 30 were waited for; matrix products, arithmetic and copies ran while one was open for 0% of the time, Pallas kernels for 0%

commit v1 on v0

--- a/solution.py
+++ b/solution.py
@@ -1,6 +1,10 @@
+import functools
+
 import jax
 import jax.numpy as jnp
 from jax import lax
+from jax.experimental import pallas as pl
+from jax.experimental.pallas import tpu as pltpu
 from jax.sharding import PartitionSpec as P
 
 SUBSTEPS = 3
@@ -34,7 +38,7 @@
     return total
 
 
-def on_device(depth, rainfall, conveyance, flow_dir, outlet):
+def on_device_tiles(depth, rainfall, conveyance, flow_dir, outlet):
     route = jnp.where(outlet == 1, 0, flow_dir + 1)
     length = jnp.where(flow_dir % 2 == 1, jnp.float32(0.70710678), jnp.float32(1.0))
     route_pad = extended(route, (("row", 0), ("col", 1)), 1)
@@ -70,6 +74,268 @@
     return (level, jnp.log(1.0 + acc))
 
 
+LANES = 128
+HALF = LANES // 2
+SUB = 8
+FIELDS = 4
+SPARE = LANES // FIELDS
+UNROLL = 2
+
+
+def lane_of():
+    return lax.broadcasted_iota(jnp.int32, (SUB, LANES), 1)
+
+
+def coded(conveyance, flow_dir, outlet):
+    length = jnp.where((flow_dir & 1) == 1, jnp.float32(0.70710678), jnp.float32(1.0))
+    route = jnp.where(outlet == 1, 0, flow_dir + 1).astype(jnp.float32)
+    return conveyance * length, route
+
+
+def edge_kernel(*refs):
+    rows = refs[0].shape[0]
+    for side in range(2):
+        depth, rain, conv, code, outlet = (ref[...] for ref in refs[5 * side : 5 * side + 5])
+        factor, route = coded(conv, code, outlet)
+        out = refs[10 + side]
+        for f, value in enumerate((depth, rain, factor, route)):
+            out[pl.ds(f * rows, rows), :] = value
+
+
+def pack_kernel(peers, flags, depth, rain, conv, code, outlet, before, after, out):
+    rows = depth.shape[0]
+    lane = lax.broadcasted_iota(jnp.int32, (rows, LANES), 1)
+    left = flags[0].astype(jnp.float32)
+    right = flags[1].astype(jnp.float32)
+    tiles = []
+    first = [before[pl.ds(f * rows, rows), :] for f in range(FIELDS)]
+    first[3] = first[3] * left
+    tiles.append(first)
+    for q in range(peers):
+        cut = pl.ds(q * LANES, LANES)
+        factor, route = coded(conv[:, cut], code[:, cut], outlet[:, cut])
+        tiles.append([depth[:, cut], rain[:, cut], factor, route])
+    last = [after[pl.ds(f * rows, rows), :] for f in range(FIELDS)]
+    last[3] = last[3] * right
+    tiles.append(last)
+    for q in range(peers):
+        spare = None
+        for f in range(FIELDS):
+            prev, own, following = tiles[q][f], tiles[q + 1][f], tiles[q + 2][f]
+            out[q, pl.ds(2 * f * rows, rows), :] = own
+            out[q, pl.ds((2 * f + 1) * rows, rows), :] = jnp.where(lane < HALF, following, prev)
+            third = jnp.where(lane < HALF, prev, following)
+            moved = pltpu.roll(third, (SPARE * f - HALF + SPARE // 2) % LANES, 1)
+            spare = moved if spare is None else jnp.where(lane >= SPARE * f, moved, spare)
+        out[q, pl.ds(2 * FIELDS * rows, rows), :] = spare
+
+
+def shifted(tiles, lane, step):
+    turned = [pltpu.roll(tile, step % LANES, 1) for tile in tiles]
+    wrap = 0 if step == 1 else LANES - 1
+    seam = HALF if step == 1 else HALF - 1
+    own = jnp.where(lane == wrap, turned[1], turned[0])
+    near = jnp.where(lane == wrap, turned[0], turned[1])
+    if len(tiles) == 2:
+        return [own, near]
+    return [own, jnp.where(lane == seam, turned[2], near), jnp.where(lane == seam, turned[1], turned[2])]
+
+
+def parts(masks, q, values, lane):
+    count = len(values)
+    east, west = shifted(values, lane, 1), shifted(values, lane, -1)
+    here, down, above = [], [], []
+    for t in range(count):
+        v, e, w = values[t], east[t], west[t]
+        m = [masks[k, q, t] for k in range(8)]
+        here.append(m[0] * e + m[4] * w)
+        down.append((m[1] * e + m[3] * w) + m[2] * v)
+        above.append((m[7] * e + m[5] * w) + m[6] * v)
+    return here, down, above
+
+
+def sweep(masks, rows, count, lane, value, base, store):
+    held = None
+    for q in range(rows):
+        here, down, above = parts(masks, q, value(q), lane)
+        mine = [b + h for b, h in zip(base(q), here)]
+        if q == 0:
+            wrapped = [pltpu.roll(a, SUB - 1, 0) for a in above]
+        else:
+            done = [p + a for p, a in zip(pending, above)]
+            if q == 1:
+                held = done
+            else:
+                store(q - 1, done)
+            mine = [p + d for p, d in zip(mine, carried)]
+        pending, carried = mine, down
+    store(rows - 1, [p + a for p, a in zip(pending, wrapped)])
+    store(0, [p + pltpu.roll(d, 1, 0) for p, d in zip(held, carried)])
+
+
+def strip_kernel(peers, got, out, flat, masks, rain, conv, level, total, final):
+    block = got.shape[1] // (2 * FIELDS + 1)
+    height = peers * block
+    rows = height // SUB
+    lane = lane_of()
+    sub = lax.broadcasted_iota(jnp.int32, (SUB, LANES), 0)
+    for p in range(peers):
+        for f in range(2 * FIELDS + 1):
+            flat[f, pl.ds(p * block, block), :] = got[p, pl.ds(f * block, block), :]
+
+    def prepare(q, _):
+        cut = pl.ds(q, SUB, stride=rows)
+        spare = flat[2 * FIELDS, cut, :]
+        field = []
+        for f in range(FIELDS):
+            third = pltpu.roll(spare, (HALF - SPARE // 2 - SPARE * f) % LANES, 1)
+            field.append([flat[2 * f, cut, :], flat[2 * f + 1, cut, :], third])
+        for t in range(3):
+            level[q, t] = field[0][t]
+            rain[q, t] = field[1][t]
+            conv[q, t] = field[2][t]
+        route = field[3]
+        east, west = shifted(route, lane, 1), shifted(route, lane, -1)
+        source = (east, east, route, west, west, west, route, east)
+        top = jnp.logical_and(q == 0, sub == 0)
+        bottom = jnp.logical_and(q == rows - 1, sub == SUB - 1)
+        for k in range(8):
+            di = OFFSETS[k][0]
+            for t in range(3):
+                hit = source[k][t] == jnp.float32(k + 1)
+                if di == 1:
+                    hit = jnp.logical_and(hit, jnp.logical_not(bottom))
+                if di == -1:
+                    hit = jnp.logical_and(hit, jnp.logical_not(top))
+                masks[k, q, t] = jnp.where(hit, jnp.float32(1.0), jnp.float32(0.0))
+        return 0
+
+    lax.fori_loop(0, rows, prepare, 0)
+
+    def substep(_, carry):
+        def leaving(q, _):
+            for t in range(3):
+                h = level[q, t]
+                a = conv[q, t] * jnp.exp(jnp.float32(2.0 / 3.0) * jnp.log(h))
+                o = h * (a / (1.0 + a))
+                total[q, t] = o
+                level[q, t] = h + rain[q, t] - o
+            return 0
+
+        lax.fori_loop(0, rows, leaving, 0, unroll=2)
+
+        def store(q, tiles):
+            for t in range(3):
+                level[q, t] = tiles[t]
+
+        sweep(masks, rows, 3, lane, lambda q: [total[q, t] for t in range(3)], lambda q: [level[q, t] for t in range(3)], store)
+        return carry
+
+    lax.fori_loop(0, SUBSTEPS, substep, 0)
+
+    def begin(q, _):
+        for t in range(2):
+            total[q, t] = level[q, t]
+        final[0, pl.ds(q, SUB, stride=rows), :] = level[q, 0]
+        return 0
+
+    lax.fori_loop(0, rows, begin, 0, unroll=2)
+
+    def store(q, tiles):
+        for t in range(2):
+            total[q, t] = tiles[t]
+
+    def several(_, carry):
+        for _ in range(UNROLL):
+            sweep(masks, rows, 2, lane, lambda q: [total[q, t] for t in range(2)], lambda q: [level[q, t] for t in range(2)], store)
+        return carry
+
+    lax.fori_loop(0, PASSES // UNROLL, several, 0)
+
+    def finish(q, _):
+        final[1, pl.ds(q, SUB, stride=rows), :] = jnp.log(1.0 + total[q, 0])
+        return 0
+
+    lax.fori_loop(0, rows, finish, 0, unroll=2)
+    for p in range(peers):
+        for f in range(2):
+            out[p, pl.ds(f * block, block), :] = final[f, pl.ds(p * block, block), :]
+
+
+def join_kernel(peers, got, depth, discharge):
+    rows = depth.shape[0]
+    for q in range(peers):
+        depth[:, pl.ds(q * LANES, LANES)] = got[q, pl.ds(0, rows), :]
+        discharge[:, pl.ds(q * LANES, LANES)] = got[q, pl.ds(rows, rows), :]
+
+
+def on_device_strips(depth, rainfall, conveyance, flow_dir, outlet):
+    args = (depth, rainfall, conveyance, flow_dir, outlet)
+    rows, cols = depth.shape
+    peers, across = lax.axis_size("row"), lax.axis_size("col")
+    place = lax.axis_index("col")
+    vmem = pl.BlockSpec(memory_space=pltpu.VMEM)
+    f32 = jnp.float32
+    first = pl.BlockSpec((rows, LANES), lambda i: (0, 0))
+    last = pl.BlockSpec((rows, LANES), lambda i: (0, cols // LANES - 1))
+    edge = jax.ShapeDtypeStruct((FIELDS * rows, LANES), f32)
+    low, high = pl.pallas_call(
+        edge_kernel,
+        grid=(1,),
+        in_specs=[first] * 5 + [last] * 5,
+        out_specs=[pl.BlockSpec((FIELDS * rows, LANES), lambda i: (0, 0))] * 2,
+        out_shape=[edge, edge],
+        name="edges",
+    )(*args, *args)
+    ring = [(i, (i + 1) % across) for i in range(across)]
+    before = lax.ppermute(high, "col", ring)
+    after = lax.ppermute(low, "col", [(j, i) for i, j in ring])
+    flags = jnp.stack([place > 0, place < across - 1]).astype(jnp.int32)
+    size = 2 * FIELDS + 1
+    packed = pl.pallas_call(
+        functools.partial(pack_kernel, peers),
+        in_specs=[pl.BlockSpec(memory_space=pltpu.SMEM)] + [vmem] * 7,
+        out_specs=vmem,
+        out_shape=jax.ShapeDtypeStruct((peers, size * rows, LANES), f32),
+        name="pack",
+    )(flags, *args, before, after)
+    got = lax.all_to_all(packed, "row", 0, 0, tiled=True)
+    height = peers * rows
+    tall = height // SUB
+    made = pl.pallas_call(
+        functools.partial(strip_kernel, peers),
+        in_specs=[vmem],
+        out_specs=vmem,
+        out_shape=jax.ShapeDtypeStruct((peers, 2 * rows, LANES), f32),
+        scratch_shapes=[
+            pltpu.VMEM((size, height, LANES), f32),
+            pltpu.VMEM((8, tall, 3, SUB, LANES), f32),
+            pltpu.VMEM((tall, 3, SUB, LANES), f32),
+            pltpu.VMEM((tall, 3, SUB, LANES), f32),
+            pltpu.VMEM((tall, 3, SUB, LANES), f32),
+            pltpu.VMEM((tall, 3, SUB, LANES), f32),
+            pltpu.VMEM((2, height, LANES), f32),
+        ],
+        name="strip",
+    )(got)
+    back = lax.all_to_all(made, "row", 0, 0, tiled=True)
+    whole = jax.ShapeDtypeStruct((rows, cols), f32)
+    return pl.pallas_call(
+        functools.partial(join_kernel, peers),
+        in_specs=[vmem],
+        out_specs=[vmem, vmem],
+        out_shape=[whole, whole],
+        name="join",
+    )(back)
+
+
+def on_device(*args):
+    rows, cols = args[0].shape
+    peers = lax.axis_size("row")
+    fits = cols == peers * LANES and rows % SUB == 0 and PASSES <= HALF and SUBSTEPS <= SPARE // 2
+    return tuple((on_device_strips if fits else on_device_tiles)(*args))
+
+
 def solution(mesh):
     placed = (P("row", "col"), P("row", "col"), P("row", "col"), P("row", "col"), P("row", "col"))
     return jax.shard_map(

time: 267 us -> 70.4 us (0.26); the launches traced: 262 us -> 70 us
  starting transfers between devices: 148 us -> 4.54 us
  waiting for transfers between devices: 56.4 us -> 2.26 us
  other arithmetic: 54.4 us -> 0.66 us
  blocking collectives: 0 us -> 30.9 us
  Pallas kernels: 0 us -> 29.7 us
    ppermute x56 -> x2, starting transfers between devices: 148 us -> 4.54 us  [the longest x1 4.05 us: on_device_strips(): after = lax.ppermute(low, 'col', [(j, i) for i, j in ring])]
    ppermute x56 -> x2, waiting for transfers between devices: 56.4 us -> 2.26 us  [the longest x1 2.26 us: on_device_strips(): before = lax.ppermute(high, 'col', ring)]
    select_n x67 -> x0, other arithmetic: 48.1 us -> none  [the longest x64 45.4 us: group_pass(): sent = jnp.where(route_here > 0, current, jnp.float32(0.0))]
    all_to_all x0 -> x2, blocking collectives: none -> 30.9 us  [the longest x1 21 us: on_device_strips(): got = lax.all_to_all(packed, 'row', 0, 0, tiled=True)]
    pallas_call x0 -> x4, Pallas kernels: none -> 29.7 us  [the longest x1 23.8 us: on_device_strips(): pl.pallas_call(functools.partial(strip_kernel, peers), in_specs=[vmem], o...]
    add x9 -> x0, other arithmetic: 4.46 us -> none  [the longest x8 4.06 us: group_pass(): current = level_here + padded_inflow(sent, route_here)]
  transfers between devices with their start and end apart: 56 -> 2, of which waited for: 30 -> 1; matrix products, arithmetic and copies ran while one was open for 0% -> 1% of each run, Pallas kernels for 0% -> 0%
where the time goes in v1:
time: 70.4 us; the launch traced here: 70 us
  blocking collectives  30.9 us (44%)
  Pallas kernels  29.7 us (42%)
  starting transfers between devices  4.54 us (6%)
  waiting for transfers between devices  2.26 us (3%)
  local copies, waits for them, and re-layouts  1.31 us (2%)
    pallas_call x1, Pallas kernels, on_device_strips(): pl.pallas_call(functools.partial(strip_kernel, peers), in_specs=[vmem], o...  23.8 us
    all_to_all x1, blocking collectives, on_device_strips(): got = lax.all_to_all(packed, 'row', 0, 0, tiled=True)  21 us
    all_to_all x1, blocking collectives, on_device_strips(): back = lax.all_to_all(made, 'row', 0, 0, tiled=True)  9.93 us
    ppermute x1, starting transfers between devices, on_device_strips(): after = lax.ppermute(low, 'col', [(j, i) for i, j in ring])  4.05 us
    pallas_call x1, Pallas kernels, on_device_strips(): pl.pallas_call(functools.partial(pack_kernel, peers), in_specs=[pl.BlockS...  2.5 us
    ppermute x1, waiting for transfers between devices, on_device_strips(): before = lax.ppermute(high, 'col', ring)  2.26 us
    pallas_call x1, Pallas kernels, on_device_strips(): pl.pallas_call(functools.partial(join_kernel, peers), in_specs=[vmem], ou...  1.67 us
    pallas_call x1, Pallas kernels, on_device_strips(): pl.pallas_call(edge_kernel, grid=(1,), in_specs=[first] * 5 + [last] * 5,...  1.64 us
  transfers between devices with their start and end apart: 2, of which 1 were waited for; matrix products, arithmetic and copies ran while one was open for 1% of the time, Pallas kernels for 0%

profile of v1, /device:TPU:0, one launch (start us, length us, event | category | flops | bytes accessed | tf_op | source)
XLA Modules:
  0.0 70.0 jit_solution(17617537345384155077)
XLA Ops:
  0.6 1.6 %edges.1 = (f32[256,128]{1,0:T(8,128)}, f32[256,128]{1,0:T(8,128)}) custom-call(f32[64,512]{1,0:T(8,128)} %depth.1, f32[64,512]{1,0:T(8,128)} %rain.1, f32[64,512]{1,0:T(8,128)} %conv.1, s32[64,512]{1,0:T(8,128)} %code.1, s32[64,512]{1,0:T(8,128)} %outlet.1, f32[64,512]{1,0:T(8,128)} %depth.1, f32[64,512]{1,0:T(8,128)} %rain.1, f32[64,512]{1,0:T(8,128)} %conv.1, ...), custom_call_target="tpu_custom_call" | custom-call | tf_op jit(solution)/shard_map/edges/pallas_call | solution.py:282
  2.3 0.5 collective-permute-start
  2.8 4.1 %collective-permute-start.1 = (f32[256,128]{1,0:T(8,128)}, f32[256,128]{1,0:T(8,128)S(1)}, u32[]{:S(2)}, u32[]{:S(2)}) collective-permute-start(f32[256,128]{1,0:T(8,128)} %get-tuple-element.5), channel_id=1, source_target_pairs={{1,0},{2,1},{3,2},{4,3},{5,4},{6,5},{7,6},{0,7},{9,8},{10,9},{11,1... | collective-permute-start | bytes 393224 | tf_op jit(solution)/shard_map/ppermute | solution.py:292
  6.8 0.7 add_convert_fusion.flags
  7.5 2.3 %collective-permute-done.before = f32[256,128]{1,0:T(8,128)S(1)} collective-permute-done((f32[256,128]{1,0:T(8,128)}, f32[256,128]{1,0:T(8,128)S(1)}, u32[]{:S(2)}, u32[]{:S(2)}) %collective-permute-start) | collective-permute-done | bytes 131104 | tf_op jit(solution)/shard_map/ppermute | solution.py:291
  9.7 0.0 copy-start
  9.7 0.0 collective-permute-done.1.after
  9.7 0.7 copy-done
  10.4 0.0 copy-start.1
  10.4 0.7 copy-done.1
  11.1 2.5 %pack.1 = f32[4,576,128]{2,1,0:T(8,128)} custom-call(s32[2]{0:T(128)} %add_convert_fusion.flags, f32[64,512]{1,0:T(8,128)} %depth.1, f32[64,512]{1,0:T(8,128)} %rain.1, f32[64,512]{1,0:T(8,128)} %conv.1, s32[64,512]{1,0:T(8,128)} %code.1, s32[64,512]{1,0:T(8,128)} %outlet.1, f32[256,128]{1,0:T(8,128)} %copy-done, f32[256,128]{1,0:T(8,128)} %copy-done.1), custom_call_target="tpu_custom_call" | custom-call | tf_op jit(solution)/shard_map/pack/pallas_call | solution.py:295
  13.6 21.0 %all_to_all.10.got = f32[4,576,128]{2,1,0:T(8,128)} all-to-all(f32[4,576,128]{2,1,0:T(8,128)} %pack.1), channel_id=1, replica_groups=mesh['row'=4,'col'=8] {'row'}, dimensions={0} | all-to-all | bytes 2359296 | tf_op jit(solution)/shard_map/all_to_all | solution.py:302
  34.6 23.8 %strip.1 = f32[4,128,128]{2,1,0:T(8,128)} custom-call(f32[4,576,128]{2,1,0:T(8,128)} %all_to_all.10.got), custom_call_target="tpu_custom_call" | custom-call | tf_op jit(solution)/shard_map/strip/pallas_call | solution.py:305
  58.4 9.9 %all_to_all.11.got = f32[4,128,128]{2,1,0:T(8,128)} all-to-all(f32[4,128,128]{2,1,0:T(8,128)} %strip.1), channel_id=1, replica_groups=mesh['row'=4,'col'=8] {'row'}, dimensions={0} | all-to-all | bytes 524288 | tf_op jit(solution)/shard_map/all_to_all | solution.py:321
  68.3 1.7 %join.1 = (f32[64,512]{1,0:T(8,128)}, f32[64,512]{1,0:T(8,128)}) custom-call(f32[4,128,128]{2,1,0:T(8,128)} %all_to_all.11.got), custom_call_target="tpu_custom_call" | custom-call | tf_op jit(solution)/shard_map/join/pallas_call | solution.py:323
Async XLA Ops:
  2.3 7.5 %collective-permute-start = (f32[256,128]{1,0:T(8,128)}, f32[256,128]{1,0:T(8,128)S(1)}, u32[]{:S(2)}, u32[]{:S(2)}) collective-permute-start(f32[256,128]{1,0:T(8,128)} %get-tuple-element.4), channel_id=1, source_target_pairs={{0,1},{1,2},{2,3},{3,4},{4,5},{5,6},{6,7},{7,0},{8,9},{9,10},{10,1... | collective-permute-start | bytes 393224 | tf_op jit(solution)/shard_map/ppermute | solution.py:291
  2.8 7.0 %collective-permute-start.1 = (f32[256,128]{1,0:T(8,128)}, f32[256,128]{1,0:T(8,128)S(1)}, u32[]{:S(2)}, u32[]{:S(2)}) collective-permute-start(f32[256,128]{1,0:T(8,128)} %get-tuple-element.5), channel_id=1, source_target_pairs={{1,0},{2,1},{3,2},{4,3},{5,4},{6,5},{7,6},{0,7},{9,8},{10,9},{11,1... | collective-permute-start | bytes 393224 | tf_op jit(solution)/shard_map/ppermute | solution.py:292
  9.7 0.7 copy-start
  10.4 0.7 copy-start.1

commit v2 on v1

--- a/solution.py
+++ b/solution.py
@@ -80,6 +80,7 @@
 FIELDS = 4
 SPARE = LANES // FIELDS
 UNROLL = 2
+PAD = SUB
 
 
 def lane_of():
@@ -102,11 +103,12 @@
             out[pl.ds(f * rows, rows), :] = value
 
 
-def pack_kernel(peers, flags, depth, rain, conv, code, outlet, before, after, out):
+def pack_kernel(peers, across, depth, rain, conv, code, outlet, before, after, out):
     rows = depth.shape[0]
     lane = lax.broadcasted_iota(jnp.int32, (rows, LANES), 1)
-    left = flags[0].astype(jnp.float32)
-    right = flags[1].astype(jnp.float32)
+    place = lax.axis_index("col")
+    left = jnp.where(place > 0, jnp.float32(1.0), jnp.float32(0.0))
+    right = jnp.where(place < across - 1, jnp.float32(1.0), jnp.float32(0.0))
     tiles = []
     first = [before[pl.ds(f * rows, rows), :] for f in range(FIELDS)]
     first[3] = first[3] * left
@@ -179,12 +181,15 @@
     rows = height // SUB
     lane = lane_of()
     sub = lax.broadcasted_iota(jnp.int32, (SUB, LANES), 0)
+    pitch = rows + PAD
+    share = SUB // peers
     for p in range(peers):
-        for f in range(2 * FIELDS + 1):
-            flat[f, pl.ds(p * block, block), :] = got[p, pl.ds(f * block, block), :]
+        for g in range(share):
+            for f in range(2 * FIELDS + 1):
+                flat[f, pl.ds((p * share + g) * pitch, rows), :] = got[p, pl.ds(f * block + g * rows, rows), :]
 
     def prepare(q, _):
-        cut = pl.ds(q, SUB, stride=rows)
+        cut = pl.ds(q, SUB, stride=pitch)
         spare = flat[2 * FIELDS, cut, :]
         field = []
         for f in range(FIELDS):
@@ -210,7 +215,7 @@
                 masks[k, q, t] = jnp.where(hit, jnp.float32(1.0), jnp.float32(0.0))
         return 0
 
-    lax.fori_loop(0, rows, prepare, 0)
+    lax.fori_loop(0, rows, prepare, 0, unroll=8)
 
     def substep(_, carry):
         def leaving(q, _):
@@ -222,7 +227,7 @@
                 level[q, t] = h + rain[q, t] - o
             return 0
 
-        lax.fori_loop(0, rows, leaving, 0, unroll=2)
+        lax.fori_loop(0, rows, leaving, 0, unroll=8)
 
         def store(q, tiles):
             for t in range(3):
@@ -236,10 +241,10 @@
     def begin(q, _):
         for t in range(2):
             total[q, t] = level[q, t]
-        final[0, pl.ds(q, SUB, stride=rows), :] = level[q, 0]
+        final[0, pl.ds(q, SUB, stride=pitch), :] = level[q, 0]
         return 0
 
-    lax.fori_loop(0, rows, begin, 0, unroll=2)
+    lax.fori_loop(0, rows, begin, 0, unroll=8)
 
     def store(q, tiles):
         for t in range(2):
@@ -253,13 +258,14 @@
     lax.fori_loop(0, PASSES // UNROLL, several, 0)
 
     def finish(q, _):
-        final[1, pl.ds(q, SUB, stride=rows), :] = jnp.log(1.0 + total[q, 0])
+        final[1, pl.ds(q, SUB, stride=pitch), :] = jnp.log(1.0 + total[q, 0])
         return 0
 
-    lax.fori_loop(0, rows, finish, 0, unroll=2)
+    lax.fori_loop(0, rows, finish, 0, unroll=8)
     for p in range(peers):
-        for f in range(2):
-            out[p, pl.ds(f * block, block), :] = final[f, pl.ds(p * block, block), :]
+        for g in range(share):
+            for f in range(2):
+                out[p, pl.ds(f * block + g * rows, rows), :] = final[f, pl.ds((p * share + g) * pitch, rows), :]
 
 
 def join_kernel(peers, got, depth, discharge):
@@ -273,7 +279,6 @@
     args = (depth, rainfall, conveyance, flow_dir, outlet)
     rows, cols = depth.shape
     peers, across = lax.axis_size("row"), lax.axis_size("col")
-    place = lax.axis_index("col")
     vmem = pl.BlockSpec(memory_space=pltpu.VMEM)
     f32 = jnp.float32
     first = pl.BlockSpec((rows, LANES), lambda i: (0, 0))
@@ -290,15 +295,14 @@
     ring = [(i, (i + 1) % across) for i in range(across)]
     before = lax.ppermute(high, "col", ring)
     after = lax.ppermute(low, "col", [(j, i) for i, j in ring])
-    flags = jnp.stack([place > 0, place < across - 1]).astype(jnp.int32)
     size = 2 * FIELDS + 1
     packed = pl.pallas_call(
-        functools.partial(pack_kernel, peers),
-        in_specs=[pl.BlockSpec(memory_space=pltpu.SMEM)] + [vmem] * 7,
+        functools.partial(pack_kernel, peers, across),
+        in_specs=[vmem] * 7,
         out_specs=vmem,
         out_shape=jax.ShapeDtypeStruct((peers, size * rows, LANES), f32),
         name="pack",
-    )(flags, *args, before, after)
+    )(*args, before, after)
     got = lax.all_to_all(packed, "row", 0, 0, tiled=True)
     height = peers * rows
     tall = height // SUB
@@ -308,13 +312,13 @@
         out_specs=vmem,
         out_shape=jax.ShapeDtypeStruct((peers, 2 * rows, LANES), f32),
         scratch_shapes=[
-            pltpu.VMEM((size, height, LANES), f32),
+            pltpu.VMEM((size, height + SUB * PAD, LANES), f32),
             pltpu.VMEM((8, tall, 3, SUB, LANES), f32),
             pltpu.VMEM((tall, 3, SUB, LANES), f32),
             pltpu.VMEM((tall, 3, SUB, LANES), f32),
             pltpu.VMEM((tall, 3, SUB, LANES), f32),
             pltpu.VMEM((tall, 3, SUB, LANES), f32),
-            pltpu.VMEM((2, height, LANES), f32),
+            pltpu.VMEM((2, height + SUB * PAD, LANES), f32),
         ],
         name="strip",
     )(got)
@@ -332,7 +336,7 @@
 def on_device(*args):
     rows, cols = args[0].shape
     peers = lax.axis_size("row")
-    fits = cols == peers * LANES and rows % SUB == 0 and PASSES <= HALF and SUBSTEPS <= SPARE // 2
+    fits = cols == peers * LANES and SUB % peers == 0 and (peers * rows) % (SUB * SUB) == 0 and PASSES <= HALF and SUBSTEPS <= SPARE // 2
     return tuple((on_device_strips if fits else on_device_tiles)(*args))
 
 

time: 70.4 us -> 65.4 us (0.929)
  Pallas kernels: 29.7 us -> 24.6 us
    pallas_call x1, Pallas kernels: 23.8 us -> 18.8 us  [on_device_strips(): pl.pallas_call(functools.partial(strip_kernel, peers), in_specs=[vmem], o...]
  transfers between devices with their start and end apart: 2 -> 2, of which waited for: 1 -> 1; matrix products, arithmetic and copies ran while one was open for 1% -> 0% of each run, Pallas kernels for 0% -> 0%
where the time goes in v2:
time: 65.4 us; the launch traced here: 64.9 us
  blocking collectives  30.9 us (47%)
  Pallas kernels  24.6 us (38%)
  starting transfers between devices  4.54 us (7%)
  waiting for transfers between devices  2.92 us (4%)
  local copies, waits for them, and re-layouts  1.31 us (2%)
    all_to_all x1, blocking collectives, on_device_strips(): got = lax.all_to_all(packed, 'row', 0, 0, tiled=True)  21 us
    pallas_call x1, Pallas kernels, on_device_strips(): pl.pallas_call(functools.partial(strip_kernel, peers), in_specs=[vmem], o...  18.8 us
    all_to_all x1, blocking collectives, on_device_strips(): back = lax.all_to_all(made, 'row', 0, 0, tiled=True)  9.94 us
    ppermute x1, starting transfers between devices, on_device_strips(): after = lax.ppermute(low, 'col', [(j, i) for i, j in ring])  4.05 us
    ppermute x1, waiting for transfers between devices, on_device_strips(): before = lax.ppermute(high, 'col', ring)  2.92 us
    pallas_call x1, Pallas kernels, on_device_strips(): pl.pallas_call(functools.partial(pack_kernel, peers, across), in_specs=[v...  2.5 us
    pallas_call x1, Pallas kernels, on_device_strips(): pl.pallas_call(functools.partial(join_kernel, peers), in_specs=[vmem], ou...  1.67 us
    pallas_call x1, Pallas kernels, on_device_strips(): pl.pallas_call(edge_kernel, grid=(1,), in_specs=[first] * 5 + [last] * 5,...  1.64 us
  transfers between devices with their start and end apart: 2, of which 1 were waited for; matrix products, arithmetic and copies ran while one was open for 0% of the time, Pallas kernels for 0%

profile of v2, /device:TPU:0, one launch (start us, length us, event | category | flops | bytes accessed | tf_op | source)
XLA Modules:
  0.0 64.9 jit_solution(16713529846918128345)
XLA Ops:
  0.6 1.6 %edges.1 = (f32[256,128]{1,0:T(8,128)}, f32[256,128]{1,0:T(8,128)}) custom-call(f32[64,512]{1,0:T(8,128)} %depth.1, f32[64,512]{1,0:T(8,128)} %rain.1, f32[64,512]{1,0:T(8,128)} %conv.1, s32[64,512]{1,0:T(8,128)} %code.1, s32[64,512]{1,0:T(8,128)} %outlet.1, f32[64,512]{1,0:T(8,128)} %depth.1, f32[64,512]{1,0:T(8,128)} %rain.1, f32[64,512]{1,0:T(8,128)} %conv.1, ...), custom_call_target="tpu_custom_call" | custom-call | tf_op jit(solution)/shard_map/edges/pallas_call | solution.py:287
  2.3 0.5 collective-permute-start
  2.8 4.1 %collective-permute-start.1 = (f32[256,128]{1,0:T(8,128)}, f32[256,128]{1,0:T(8,128)S(1)}, u32[]{:S(2)}, u32[]{:S(2)}) collective-permute-start(f32[256,128]{1,0:T(8,128)} %get-tuple-element.5), channel_id=1, source_target_pairs={{1,0},{2,1},{3,2},{4,3},{5,4},{6,5},{7,6},{0,7},{9,8},{10,9},{11,1... | collective-permute-start | bytes 393224 | tf_op jit(solution)/shard_map/ppermute | solution.py:297
  6.8 2.9 %collective-permute-done.before = f32[256,128]{1,0:T(8,128)S(1)} collective-permute-done((f32[256,128]{1,0:T(8,128)}, f32[256,128]{1,0:T(8,128)S(1)}, u32[]{:S(2)}, u32[]{:S(2)}) %collective-permute-start) | collective-permute-done | bytes 131104 | tf_op jit(solution)/shard_map/ppermute | solution.py:296
  9.7 0.0 copy-start
  9.7 0.0 collective-permute-done.1.after
  9.7 0.7 %copy-done = f32[256,128]{1,0:T(8,128)} copy-done((f32[256,128]{1,0:T(8,128)}, f32[256,128]{1,0:T(8,128)S(1)}, u32[]{:S(2)}) %copy-start) | copy-done | bytes 131096
  10.4 0.0 copy-start.1
  10.4 0.7 %copy-done.1 = f32[256,128]{1,0:T(8,128)} copy-done((f32[256,128]{1,0:T(8,128)}, f32[256,128]{1,0:T(8,128)S(1)}, u32[]{:S(2)}) %copy-start.1) | copy-done | bytes 131096
  11.1 2.5 %pack.1 = f32[4,576,128]{2,1,0:T(8,128)} custom-call(f32[64,512]{1,0:T(8,128)} %depth.1, f32[64,512]{1,0:T(8,128)} %rain.1, f32[64,512]{1,0:T(8,128)} %conv.1, s32[64,512]{1,0:T(8,128)} %code.1, s32[64,512]{1,0:T(8,128)} %outlet.1, f32[256,128]{1,0:T(8,128)} %copy-done, f32[256,128]{1,0:T(8,128)} %copy-done.1), custom_call_target="tpu_custom_call" | custom-call | tf_op jit(solution)/shard_map/pack/pallas_call | solution.py:299
  13.6 21.0 %all_to_all.10.got = f32[4,576,128]{2,1,0:T(8,128)} all-to-all(f32[4,576,128]{2,1,0:T(8,128)} %pack.1), channel_id=1, replica_groups=mesh['row'=4,'col'=8] {'row'}, dimensions={0} | all-to-all | bytes 2359296 | tf_op jit(solution)/shard_map/all_to_all | solution.py:306
  34.5 18.8 %strip.1 = f32[4,128,128]{2,1,0:T(8,128)} custom-call(f32[4,576,128]{2,1,0:T(8,128)} %all_to_all.10.got), custom_call_target="tpu_custom_call" | custom-call | tf_op jit(solution)/shard_map/strip/pallas_call | solution.py:309
  53.3 9.9 %all_to_all.11.got = f32[4,128,128]{2,1,0:T(8,128)} all-to-all(f32[4,128,128]{2,1,0:T(8,128)} %strip.1), channel_id=1, replica_groups=mesh['row'=4,'col'=8] {'row'}, dimensions={0} | all-to-all | bytes 524288 | tf_op jit(solution)/shard_map/all_to_all | solution.py:325
  63.2 1.7 %join.1 = (f32[64,512]{1,0:T(8,128)}, f32[64,512]{1,0:T(8,128)}) custom-call(f32[4,128,128]{2,1,0:T(8,128)} %all_to_all.11.got), custom_call_target="tpu_custom_call" | custom-call | tf_op jit(solution)/shard_map/join/pallas_call | solution.py:327
Async XLA Ops:
  2.3 7.5 %collective-permute-start = (f32[256,128]{1,0:T(8,128)}, f32[256,128]{1,0:T(8,128)S(1)}, u32[]{:S(2)}, u32[]{:S(2)}) collective-permute-start(f32[256,128]{1,0:T(8,128)} %get-tuple-element.4), channel_id=1, source_target_pairs={{0,1},{1,2},{2,3},{3,4},{4,5},{5,6},{6,7},{7,0},{8,9},{9,10},{10,1... | collective-permute-start | bytes 393224 | tf_op jit(solution)/shard_map/ppermute | solution.py:296
  2.8 7.0 %collective-permute-start.1 = (f32[256,128]{1,0:T(8,128)}, f32[256,128]{1,0:T(8,128)S(1)}, u32[]{:S(2)}, u32[]{:S(2)}) collective-permute-start(f32[256,128]{1,0:T(8,128)} %get-tuple-element.5), channel_id=1, source_target_pairs={{1,0},{2,1},{3,2},{4,3},{5,4},{6,5},{7,6},{0,7},{9,8},{10,9},{11,1... | collective-permute-start | bytes 393224 | tf_op jit(solution)/shard_map/ppermute | solution.py:297
  9.7 0.7 %copy-start = (f32[256,128]{1,0:T(8,128)}, f32[256,128]{1,0:T(8,128)S(1)}, u32[]{:S(2)}) copy-start(f32[256,128]{1,0:T(8,128)S(1)} %collective-permute-done.before) | copy-start | bytes 393220
  10.4 0.7 %copy-start.1 = (f32[256,128]{1,0:T(8,128)}, f32[256,128]{1,0:T(8,128)S(1)}, u32[]{:S(2)}) copy-start(f32[256,128]{1,0:T(8,128)S(1)} %collective-permute-done.1.after) | copy-start | bytes 393220

commit v3 on v2

--- a/solution.py
+++ b/solution.py
@@ -78,9 +78,13 @@
 HALF = LANES // 2
 SUB = 8
 FIELDS = 4
-SPARE = LANES // FIELDS
 UNROLL = 2
 PAD = SUB
+
+
+def sharing(peers):
+    share = SUB // peers
+    return share, LANES // (FIELDS * share)
 
 
 def lane_of():
@@ -103,33 +107,48 @@
             out[pl.ds(f * rows, rows), :] = value
 
 
-def pack_kernel(peers, across, depth, rain, conv, code, outlet, before, after, out):
+def pack_kernel(peers, across, picks, *refs):
+    depth, rain, conv, code, outlet = refs[:5]
+    out, built, sems = refs[-3:]
     rows = depth.shape[0]
     lane = lax.broadcasted_iota(jnp.int32, (rows, LANES), 1)
     place = lax.axis_index("col")
     left = jnp.where(place > 0, jnp.float32(1.0), jnp.float32(0.0))
     right = jnp.where(place < across - 1, jnp.float32(1.0), jnp.float32(0.0))
-    tiles = []
-    first = [before[pl.ds(f * rows, rows), :] for f in range(FIELDS)]
-    first[3] = first[3] * left
-    tiles.append(first)
-    for q in range(peers):
+
+    def tile(q):
+        if q < 0 or q == peers:
+            ref, inside = (refs[5], left) if q < 0 else (refs[6], right)
+            fields = [ref[pl.ds(f * rows, rows), :] for f in range(FIELDS)]
+            fields[3] = fields[3] * inside
+            return fields
         cut = pl.ds(q * LANES, LANES)
         factor, route = coded(conv[:, cut], code[:, cut], outlet[:, cut])
-        tiles.append([depth[:, cut], rain[:, cut], factor, route])
-    last = [after[pl.ds(f * rows, rows), :] for f in range(FIELDS)]
-    last[3] = last[3] * right
-    tiles.append(last)
-    for q in range(peers):
+        return [depth[:, cut], rain[:, cut], factor, route]
+
+    share, width = sharing(peers)
+    tall = rows // share
+    copies = []
+    for n, q in enumerate(picks):
         spare = None
+        prevs, owns, followings = tile(q - 1), tile(q), tile(q + 1)
         for f in range(FIELDS):
-            prev, own, following = tiles[q][f], tiles[q + 1][f], tiles[q + 2][f]
-            out[q, pl.ds(2 * f * rows, rows), :] = own
-            out[q, pl.ds((2 * f + 1) * rows, rows), :] = jnp.where(lane < HALF, following, prev)
+            prev, own, following = prevs[f], owns[f], followings[f]
+            built[n, pl.ds(2 * f * rows, rows), :] = own
+            built[n, pl.ds((2 * f + 1) * rows, rows), :] = jnp.where(lane < HALF, following, prev)
             third = jnp.where(lane < HALF, prev, following)
-            moved = pltpu.roll(third, (SPARE * f - HALF + SPARE // 2) % LANES, 1)
-            spare = moved if spare is None else jnp.where(lane >= SPARE * f, moved, spare)
-        out[q, pl.ds(2 * FIELDS * rows, rows), :] = spare
+            moved = pltpu.roll(third, (width * f - HALF + width // 2) % LANES, 1)
+            spare = moved if spare is None else jnp.where(lane >= width * f, moved, spare)
+        folded = spare[:tall]
+        for g in range(1, share):
+            group = pltpu.roll(spare[g * tall : (g + 1) * tall], g * FIELDS * width, 1)
+            folded = jnp.where(lane[:tall] >= g * FIELDS * width, group, folded)
+        built[n, pl.ds(2 * FIELDS * rows, tall), :] = folded
+        copy = pltpu.make_async_copy(built.at[n], out.at[q], sems.at[n])
+        copy.start()
+        copies.append(copy)
+    for copy in copies:
+        copy.wait()
 
 
 def shifted(tiles, lane, step):
@@ -176,16 +195,20 @@
 
 
 def strip_kernel(peers, got, out, flat, masks, rain, conv, level, total, final):
-    block = got.shape[1] // (2 * FIELDS + 1)
+    share, width = sharing(peers)
+    block = got.shape[1] * share // (2 * FIELDS * share + 1)
     height = peers * block
     rows = height // SUB
     lane = lane_of()
     sub = lax.broadcasted_iota(jnp.int32, (SUB, LANES), 0)
     pitch = rows + PAD
-    share = SUB // peers
     for p in range(peers):
         for g in range(share):
-            for f in range(2 * FIELDS + 1):
+            kept = got[p, pl.ds(2 * FIELDS * block, rows), :]
+            if g:
+                kept = pltpu.roll(kept, LANES - g * FIELDS * width, 1)
+            flat[2 * FIELDS, pl.ds((p * share + g) * pitch, rows), :] = kept
+            for f in range(2 * FIELDS):
                 flat[f, pl.ds((p * share + g) * pitch, rows), :] = got[p, pl.ds(f * block + g * rows, rows), :]
 
     def prepare(q, _):
@@ -193,7 +216,7 @@
         spare = flat[2 * FIELDS, cut, :]
         field = []
         for f in range(FIELDS):
-            third = pltpu.roll(spare, (HALF - SPARE // 2 - SPARE * f) % LANES, 1)
+            third = pltpu.roll(spare, (HALF - width // 2 - width * f) % LANES, 1)
             field.append([flat[2 * f, cut, :], flat[2 * f + 1, cut, :], third])
         for t in range(3):
             level[q, t] = field[0][t]
@@ -296,13 +319,35 @@
     before = lax.ppermute(high, "col", ring)
     after = lax.ppermute(low, "col", [(j, i) for i, j in ring])
     size = 2 * FIELDS + 1
+    tallest = 2 * FIELDS * rows + rows // sharing(peers)[0]
+    wide = jax.ShapeDtypeStruct((peers, tallest, LANES), f32)
+    anywhere = pl.BlockSpec(memory_space=pl.ANY)
+
+    def scratch(count):
+        return [pltpu.VMEM((count, tallest, LANES), f32), pltpu.SemaphoreType.DMA((count,))]
+
+    ends = sorted({0, peers - 1})
+    inner = [q for q in range(peers) if q not in ends]
+    operands, specs, alias = (*args, before, after), [vmem] * 7, {}
+    if inner:
+        partial = pl.pallas_call(
+            functools.partial(pack_kernel, peers, across, inner),
+            in_specs=[vmem] * 5,
+            out_specs=anywhere,
+            out_shape=wide,
+            scratch_shapes=scratch(len(inner)),
+            name="packinner",
+        )(*args)
+        operands, specs, alias = operands + (partial,), specs + [anywhere], {7: 0}
     packed = pl.pallas_call(
-        functools.partial(pack_kernel, peers, across),
-        in_specs=[vmem] * 7,
-        out_specs=vmem,
-        out_shape=jax.ShapeDtypeStruct((peers, size * rows, LANES), f32),
-        name="pack",
-    )(*args, before, after)
+        functools.partial(pack_kernel, peers, across, ends),
+        in_specs=specs,
+        out_specs=anywhere,
+        out_shape=wide,
+        scratch_shapes=scratch(len(ends)),
+        input_output_aliases=alias,
+        name="packends",
+    )(*operands)
     got = lax.all_to_all(packed, "row", 0, 0, tiled=True)
     height = peers * rows
     tall = height // SUB
@@ -336,7 +381,7 @@
 def on_device(*args):
     rows, cols = args[0].shape
     peers = lax.axis_size("row")
-    fits = cols == peers * LANES and SUB % peers == 0 and (peers * rows) % (SUB * SUB) == 0 and PASSES <= HALF and SUBSTEPS <= SPARE // 2
+    fits = cols == peers * LANES and SUB % peers == 0 and rows * peers % (SUB * SUB) == 0 and PASSES <= HALF and SUBSTEPS <= sharing(peers)[1] // 2
     return tuple((on_device_strips if fits else on_device_tiles)(*args))
 
 

time: 65.4 us -> 64.7 us (0.989)
  waiting for transfers between devices: 2.92 us -> 0.76 us
  Pallas kernels: 24.6 us -> 26.5 us
    ppermute x1, waiting for transfers between devices: 2.92 us -> 0.75 us  [on_device_strips(): before = lax.ppermute(high, 'col', ring)]
    pallas_call x1 -> x2, Pallas kernels: 2.5 us -> 4.41 us  [the longest x1 2.26 us: on_device_strips(): pl.pallas_call(functools.partial(pack_kernel, peers, across, ends), in_sp...]
  transfers between devices with their start and end apart: 2 -> 2, of which waited for: 1 -> 1; matrix products, arithmetic and copies ran while one was open for 0% -> 0% of each run, Pallas kernels for 0% -> 3%
where the time goes in v3:
time: 64.7 us; the launch traced here: 64.2 us
  blocking collectives  30.4 us (47%)
  Pallas kernels  26.5 us (41%)
  starting transfers between devices  4.54 us (7%)
  local copies, waits for them, and re-layouts  1.31 us (2%)
  waiting for transfers between devices  0.76 us (1%)
  between operations  0.65 us (1%)
    all_to_all x1, blocking collectives, on_device_strips(): got = lax.all_to_all(packed, 'row', 0, 0, tiled=True)  20.6 us
    pallas_call x1, Pallas kernels, on_device_strips(): pl.pallas_call(functools.partial(strip_kernel, peers), in_specs=[vmem], o...  18.8 us
    all_to_all x1, blocking collectives, on_device_strips(): back = lax.all_to_all(made, 'row', 0, 0, tiled=True)  9.82 us
    ppermute x1, starting transfers between devices, on_device_strips(): after = lax.ppermute(low, 'col', [(j, i) for i, j in ring])  4.05 us
    pallas_call x1, Pallas kernels, on_device_strips(): pl.pallas_call(functools.partial(pack_kernel, peers, across, ends), in_sp...  2.26 us
    pallas_call x1, Pallas kernels, on_device_strips(): pl.pallas_call(functools.partial(pack_kernel, peers, across, inner), in_s...  2.16 us
    pallas_call x1, Pallas kernels, on_device_strips(): pl.pallas_call(functools.partial(join_kernel, peers), in_specs=[vmem], ou...  1.67 us
    pallas_call x1, Pallas kernels, on_device_strips(): pl.pallas_call(edge_kernel, grid=(1,), in_specs=[first] * 5 + [last] * 5,...  1.64 us
  transfers between devices with their start and end apart: 2, of which 1 were waited for; matrix products, arithmetic and copies ran while one was open for 0% of the time, Pallas kernels for 3%

profile of v3, /device:TPU:0, one launch (start us, length us, event | category | flops | bytes accessed | tf_op | source)
XLA Modules:
  0.0 64.2 jit_solution(4534423527776817076)
XLA Ops:
  0.6 1.6 %edges.1 = (f32[256,128]{1,0:T(8,128)}, f32[256,128]{1,0:T(8,128)}) custom-call(f32[64,512]{1,0:T(8,128)} %refs_0_.5, f32[64,512]{1,0:T(8,128)} %refs_1_.5, f32[64,512]{1,0:T(8,128)} %refs_2_.5, s32[64,512]{1,0:T(8,128)} %refs_3_.5, s32[64,512]{1,0:T(8,128)} %refs_4_.5, f32[64,512]{1,0:T(8,128)} %refs_0_.5, f32[64,512]{1,0:T(8,128)} %refs_1_.5, ...), custom_call_target="tpu_custom_call" | custom-call | tf_op jit(solution)/shard_map/edges/pallas_call | solution.py:310
  2.3 0.5 collective-permute-start
  2.8 4.1 %collective-permute-start.1 = (f32[256,128]{1,0:T(8,128)}, f32[256,128]{1,0:T(8,128)S(1)}, u32[]{:S(2)}, u32[]{:S(2)}) collective-permute-start(f32[256,128]{1,0:T(8,128)} %get-tuple-element.5), channel_id=1, source_target_pairs={{1,0},{2,1},{3,2},{4,3},{5,4},{6,5},{7,6},{0,7},{9,8},{10,9},{11,1... | collective-permute-start | bytes 393224 | tf_op jit(solution)/shard_map/ppermute | solution.py:320
  6.8 2.2 %packinner.1.refs_7_ = f32[4,544,128]{2,1,0:T(8,128)} custom-call(f32[64,512]{1,0:T(8,128)} %refs_0_.5, f32[64,512]{1,0:T(8,128)} %refs_1_.5, f32[64,512]{1,0:T(8,128)} %refs_2_.5, s32[64,512]{1,0:T(8,128)} %refs_3_.5, s32[64,512]{1,0:T(8,128)} %refs_4_.5), custom_call_target="tpu_custom_call" | custom-call | tf_op jit(solution)/shard_map/packinner/pallas_call | solution.py:333
  9.0 0.8 %collective-permute-done.refs_5_ = f32[256,128]{1,0:T(8,128)S(1)} collective-permute-done((f32[256,128]{1,0:T(8,128)}, f32[256,128]{1,0:T(8,128)S(1)}, u32[]{:S(2)}, u32[]{:S(2)}) %collective-permute-start) | collective-permute-done | bytes 131104 | tf_op jit(solution)/shard_map/ppermute | solution.py:319
  9.7 0.0 copy-start
  9.7 0.0 collective-permute-done.1.refs_6_
  9.7 0.7 %copy-done = f32[256,128]{1,0:T(8,128)} copy-done((f32[256,128]{1,0:T(8,128)}, f32[256,128]{1,0:T(8,128)S(1)}, u32[]{:S(2)}) %copy-start) | copy-done | bytes 131096
  10.4 0.0 copy-start.1
  10.4 0.7 %copy-done.1 = f32[256,128]{1,0:T(8,128)} copy-done((f32[256,128]{1,0:T(8,128)}, f32[256,128]{1,0:T(8,128)S(1)}, u32[]{:S(2)}) %copy-start.1) | copy-done | bytes 131096
  11.1 2.3 %packends.1 = f32[4,544,128]{2,1,0:T(8,128)} custom-call(f32[64,512]{1,0:T(8,128)} %refs_0_.5, f32[64,512]{1,0:T(8,128)} %refs_1_.5, f32[64,512]{1,0:T(8,128)} %refs_2_.5, s32[64,512]{1,0:T(8,128)} %refs_3_.5, s32[64,512]{1,0:T(8,128)} %refs_4_.5, f32[256,128]{1,0:T(8,128)} %copy-done, f32[256,128]{1,0:T(8,128)} %copy-done.1, ...), custom_call_target="tpu_custom_call", output_to_operand_aliasing={{}: (7, {})} | custom-call | tf_op jit(solution)/shard_map/packends/pallas_call | solution.py:342
  13.3 20.6 %all_to_all.10.got = f32[4,544,128]{2,1,0:T(8,128)} all-to-all(f32[4,544,128]{2,1,0:T(8,128)} %packends.1), channel_id=1, replica_groups=mesh['row'=4,'col'=8] {'row'}, dimensions={0} | all-to-all | bytes 2228224 | tf_op jit(solution)/shard_map/all_to_all | solution.py:351
  33.9 18.8 %strip.1 = f32[4,128,128]{2,1,0:T(8,128)} custom-call(f32[4,544,128]{2,1,0:T(8,128)} %all_to_all.10.got), custom_call_target="tpu_custom_call" | custom-call | tf_op jit(solution)/shard_map/strip/pallas_call | solution.py:354
  52.7 9.8 %all_to_all.11.got = f32[4,128,128]{2,1,0:T(8,128)} all-to-all(f32[4,128,128]{2,1,0:T(8,128)} %strip.1), channel_id=1, replica_groups=mesh['row'=4,'col'=8] {'row'}, dimensions={0} | all-to-all | bytes 524288 | tf_op jit(solution)/shard_map/all_to_all | solution.py:370
  62.5 1.7 %join.1 = (f32[64,512]{1,0:T(8,128)}, f32[64,512]{1,0:T(8,128)}) custom-call(f32[4,128,128]{2,1,0:T(8,128)} %all_to_all.11.got), custom_call_target="tpu_custom_call" | custom-call | tf_op jit(solution)/shard_map/join/pallas_call | solution.py:372
Async XLA Ops:
  2.3 7.5 %collective-permute-start = (f32[256,128]{1,0:T(8,128)}, f32[256,128]{1,0:T(8,128)S(1)}, u32[]{:S(2)}, u32[]{:S(2)}) collective-permute-start(f32[256,128]{1,0:T(8,128)} %get-tuple-element.4), channel_id=1, source_target_pairs={{0,1},{1,2},{2,3},{3,4},{4,5},{5,6},{6,7},{7,0},{8,9},{9,10},{10,1... | collective-permute-start | bytes 393224 | tf_op jit(solution)/shard_map/ppermute | solution.py:319
  2.8 7.0 %collective-permute-start.1 = (f32[256,128]{1,0:T(8,128)}, f32[256,128]{1,0:T(8,128)S(1)}, u32[]{:S(2)}, u32[]{:S(2)}) collective-permute-start(f32[256,128]{1,0:T(8,128)} %get-tuple-element.5), channel_id=1, source_target_pairs={{1,0},{2,1},{3,2},{4,3},{5,4},{6,5},{7,6},{0,7},{9,8},{10,9},{11,1... | collective-permute-start | bytes 393224 | tf_op jit(solution)/shard_map/ppermute | solution.py:320
  9.7 0.7 %copy-start = (f32[256,128]{1,0:T(8,128)}, f32[256,128]{1,0:T(8,128)S(1)}, u32[]{:S(2)}) copy-start(f32[256,128]{1,0:T(8,128)S(1)} %collective-permute-done.refs_5_) | copy-start | bytes 393220
  10.4 0.7 %copy-start.1 = (f32[256,128]{1,0:T(8,128)}, f32[256,128]{1,0:T(8,128)S(1)}, u32[]{:S(2)}) copy-start(f32[256,128]{1,0:T(8,128)S(1)} %collective-permute-done.1.refs_6_) | copy-start | bytes 393220
